TPU v7x, 32 devices: a whole 2x2x4 slice. The times are simulated.
32 devices in a mesh: fsdp: 16 (over z, x, core), tp: 2 (over y).
Axes of the slice: x: 2, y: 2, z: 4, core: 2. Of those that a mesh axis runs over, the one named last changes fastest.
Arguments:
- block_input: bfloat16 [3072, 2304], P(('fsdp', 'tp')), may hold values from -6 to 6
- lengths: int32 [16, 9], P('fsdp'), may hold values from 1 to 96, 192 in all within a row
- attention_norm_gain: bfloat16 [2304], P('fsdp'), may hold values from 0.25 to 1.75
- attention_post_gain: bfloat16 [2304], P('fsdp'), may hold values from 0.25 to 1.75
- feedforward_norm_gain: bfloat16 [2304], P('fsdp'), may hold values from 0.25 to 1.75
- feedforward_post_gain: bfloat16 [2304], P('fsdp'), may hold values from 0.25 to 1.75
- query_weight: bfloat16 [2304, 2048], P('fsdp', 'tp'), may hold values from -0.125 to 0.125
- key_weight: bfloat16 [2304, 1024], P('fsdp', 'tp'), may hold values from -0.125 to 0.125
- value_weight: bfloat16 [2304, 1024], P('fsdp', 'tp'), may hold values from -0.125 to 0.125
- output_weight: bfloat16 [2304, 2048], P('fsdp', 'tp'), may hold values from -0.125 to 0.125
- gate_weight: bfloat16 [2304, 9216], P('fsdp', 'tp'), may hold values from -0.125 to 0.125
- up_weight: bfloat16 [2304, 9216], P('fsdp', 'tp'), may hold values from -0.125 to 0.125
- down_weight: bfloat16 [2304, 9216], P('fsdp', 'tp'), may hold values from -0.0625 to 0.0625
- output_cotangent: bfloat16 [3072, 2304], P(('fsdp', 'tp')), may hold values from -6 to 6
Outputs:
- block_output: bfloat16 [3072, 2304], P(('fsdp', 'tp'))
- input_gradient: float32 [3072, 2304], P(('fsdp', 'tp'))
- attention_norm_gain_gradient: float32 [2304], P('fsdp')
- attention_post_gain_gradient: float32 [2304], P('fsdp')
- feedforward_norm_gain_gradient: float32 [2304], P('fsdp')
- feedforward_post_gain_gradient: float32 [2304], P('fsdp')
- query_weight_gradient: float32 [2304, 2048], P('fsdp', 'tp')
- key_weight_gradient: float32 [2304, 1024], P('fsdp', 'tp')
- value_weight_gradient: float32 [2304, 1024], P('fsdp', 'tp')
- output_weight_gradient: float32 [2304, 2048], P('fsdp', 'tp')
- gate_weight_gradient: float32 [2304, 9216], P('fsdp', 'tp')
- up_weight_gradient: float32 [2304, 9216], P('fsdp', 'tp')
- down_weight_gradient: float32 [2304, 9216], P('fsdp', 'tp')
Inputs may be any that keep to these rules, and one draw needn't show every extreme that they name: `lengths`: row g gives the length of group g's prompt (column 0) and of its 8 continuations; each row sums to 192, and its largest entry is 96.
All inputs are finite; a program needn't handle non-finite values.
Results may differ from a plain program's by a relative error of at most 0.017.
Values may be sent and summed in bfloat16 or wider, within the bound.
A program may use at most 512 MiB of HBM per device.

v0:
```python
import math
import jax
import jax.numpy as jnp
from jax import lax
from jax.sharding import PartitionSpec as P

HEAD_SIZE = 256
EPSILON = 1e-06
SOFTCAP = 50.0
NEGATIVE = -1e30


def contract_last(left_rows, right_rows):
    return lax.dot_general(
        left_rows, right_rows, (((1,), (1,)), ((), ())), preferred_element_type=jnp.float32
    )


def contract_first(left_rows, right_rows):
    return lax.dot_general(
        left_rows, right_rows, (((0,), (0,)), ((), ())), preferred_element_type=jnp.float32
    )


def normalize_parts(value_rows):
    inverse = lax.rsqrt(jnp.mean(value_rows * value_rows, axis=-1, keepdims=True) + EPSILON)
    return (value_rows * inverse, inverse)


def norm_backward(unit_rows, inverse, norm_gain, upstream):
    scaled = upstream * norm_gain
    return inverse * (scaled - unit_rows * jnp.mean(scaled * unit_rows, axis=-1, keepdims=True))


def layout(lengths_row, grouped_rows):
    segment_ends = jnp.cumsum(lengths_row)
    segment_starts = segment_ends - lengths_row
    row_index = jnp.arange(grouped_rows, dtype=jnp.int32)
    segment = jnp.sum((row_index[:, None] >= segment_ends[None, :]).astype(jnp.int32), axis=1)
    onehot = segment[:, None] == jnp.arange(lengths_row.shape[0], dtype=jnp.int32)[None, :]
    segment_begin = jnp.sum(jnp.where(onehot, segment_starts[None, :], 0), axis=1)
    prompt_shift = jnp.where(segment > 0, lengths_row[0], 0)
    return (segment, row_index - segment_begin + prompt_shift)


def rotary_tables(position):
    frequency = jnp.exp(
        jnp.arange(HEAD_SIZE // 2, dtype=jnp.float32) * (-2.0 * math.log(10000.0) / HEAD_SIZE)
    )
    angles = position.astype(jnp.float32)[:, None] * frequency[None, :]
    return (jnp.cos(angles), jnp.sin(angles))


def apply_rotary(value_rows, cosine_lookup, sine_lookup):
    half_width = value_rows.shape[-1] // 2
    first_half = value_rows[..., :half_width]
    second_half = value_rows[..., half_width:]
    cosine_part = cosine_lookup[:, None, :]
    sine_part = sine_lookup[:, None, :]
    return jnp.concatenate(
        [
            first_half * cosine_part - second_half * sine_part,
            second_half * cosine_part + first_half * sine_part,
        ],
        axis=-1,
    )


def unrotate(value_rows, cosine_lookup, sine_lookup):
    half_width = value_rows.shape[-1] // 2
    first_half = value_rows[..., :half_width]
    second_half = value_rows[..., half_width:]
    cosine_part = cosine_lookup[:, None, :]
    sine_part = sine_lookup[:, None, :]
    return jnp.concatenate(
        [
            first_half * cosine_part + second_half * sine_part,
            second_half * cosine_part - first_half * sine_part,
        ],
        axis=-1,
    )


def visible(segment):
    row_index = jnp.arange(segment.shape[0], dtype=jnp.int32)
    same_segment = (segment[:, None] == segment[None, :]) & (
        row_index[None, :] <= row_index[:, None]
    )
    from_prompt = (segment[None, :] == 0) & (segment[:, None] > 0)
    return same_segment | from_prompt


def masked_scores(rotated_query, rotated_key, visible_mask):
    raw_scores = jnp.einsum(
        "qgrd,kgd->grqk", rotated_query, rotated_key, preferred_element_type=jnp.float32
    )
    tanh_value = jnp.tanh(raw_scores * HEAD_SIZE ** (-0.5) / SOFTCAP)
    return (jnp.where(visible_mask[None, None], SOFTCAP * tanh_value, NEGATIVE), tanh_value)


def gelu_product(gate_value, up_value):
    return jax.nn.gelu(gate_value, approximate=True) * up_value


def shards(
    block_input,
    lengths,
    attention_norm_gain,
    attention_post_gain,
    feedforward_norm_gain,
    feedforward_post_gain,
    query_weight,
    key_weight,
    value_weight,
    output_weight,
    gate_weight,
    up_weight,
    down_weight,
    output_cotangent,
):
    query_full, key_full, value_full, output_full, gain_one, gain_two = (
        lax.all_gather(query_weight, "fsdp", axis=0, tiled=True),
        lax.all_gather(key_weight, "fsdp", axis=0, tiled=True),
        lax.all_gather(value_weight, "fsdp", axis=0, tiled=True),
        lax.all_gather(output_weight, "fsdp", axis=0, tiled=True),
        lax.all_gather(attention_norm_gain, "fsdp", axis=0, tiled=True),
        lax.all_gather(attention_post_gain, "fsdp", axis=0, tiled=True),
    )
    gate_full, up_full, down_full, gain_three, gain_four = (
        lax.all_gather(gate_weight, "fsdp", axis=0, tiled=True),
        lax.all_gather(up_weight, "fsdp", axis=0, tiled=True),
        lax.all_gather(down_weight, "fsdp", axis=0, tiled=True),
        lax.all_gather(feedforward_norm_gain, "fsdp", axis=0, tiled=True),
        lax.all_gather(feedforward_post_gain, "fsdp", axis=0, tiled=True),
    )
    gain_one = gain_one.astype(jnp.float32)
    gain_two = gain_two.astype(jnp.float32)
    gain_three = gain_three.astype(jnp.float32)
    gain_four = gain_four.astype(jnp.float32)
    rows_local = block_input.shape[0]
    grouped_rows = rows_local * lax.axis_size("tp")
    segment, position = layout(lengths[0], grouped_rows)
    cosine_lookup, sine_lookup = rotary_tables(position)
    visible_mask = visible(segment)
    residual = block_input.astype(jnp.float32)
    unit_one, inverse_one = normalize_parts(residual)
    normed_local = (unit_one * gain_one).astype(jnp.bfloat16)
    normed = lax.all_gather(normed_local, "tp", axis=0, tiled=True)
    query_raw = jnp.dot(normed, query_full, preferred_element_type=jnp.float32)
    key_raw = jnp.dot(normed, key_full, preferred_element_type=jnp.float32)
    value_raw = jnp.dot(normed, value_full, preferred_element_type=jnp.float32)
    heads_local = query_raw.shape[1] // HEAD_SIZE
    kv_local = key_raw.shape[1] // HEAD_SIZE
    repeat_heads = heads_local // kv_local
    rotated_query = apply_rotary(
        query_raw.reshape(grouped_rows, heads_local, HEAD_SIZE), cosine_lookup, sine_lookup
    ).astype(jnp.bfloat16)
    rotated_query = rotated_query.reshape(grouped_rows, kv_local, repeat_heads, HEAD_SIZE)
    rotated_key = apply_rotary(
        key_raw.reshape(grouped_rows, kv_local, HEAD_SIZE), cosine_lookup, sine_lookup
    ).astype(jnp.bfloat16)
    value_reduced = value_raw.astype(jnp.bfloat16).reshape(grouped_rows, kv_local, HEAD_SIZE)
    capped, tanh_value = masked_scores(rotated_query, rotated_key, visible_mask)
    row_peak = jnp.max(capped, axis=-1, keepdims=True)
    log_total = row_peak + jnp.log(jnp.sum(jnp.exp(capped - row_peak), axis=-1, keepdims=True))
    softmax_probs = jnp.exp(capped - log_total)
    mixed_heads = jnp.einsum(
        "grqk,kgd->qgrd",
        softmax_probs.astype(jnp.bfloat16),
        value_reduced,
        preferred_element_type=jnp.float32,
    )
    attended = mixed_heads.reshape(grouped_rows, heads_local * HEAD_SIZE).astype(jnp.bfloat16)
    row_piece = attended
    branch_one = lax.psum_scatter(
        contract_last(row_piece, output_full), "tp", scatter_dimension=0, tiled=True
    )
    unit_two, inverse_two = normalize_parts(branch_one)
    middle = residual + unit_two * gain_two
    unit_three, inverse_three = normalize_parts(middle)
    feed_local = (unit_three * gain_three).astype(jnp.bfloat16)
    feed_input = lax.all_gather(feed_local, "tp", axis=0, tiled=True)
    gate_value = jnp.dot(feed_input, gate_full, preferred_element_type=jnp.float32)
    up_value = jnp.dot(feed_input, up_full, preferred_element_type=jnp.float32)
    hidden = gelu_product(gate_value, up_value).astype(jnp.bfloat16)
    row_piece = hidden
    branch_two = lax.psum_scatter(
        contract_last(row_piece, down_full), "tp", scatter_dimension=0, tiled=True
    )
    unit_four, inverse_four = normalize_parts(branch_two)
    block_output = (middle + unit_four * gain_four).astype(jnp.bfloat16)
    upstream = output_cotangent.astype(jnp.float32)
    gain_four_grad = jnp.sum(upstream * unit_four, axis=0)
    branch_two_grad = norm_backward(unit_four, inverse_four, gain_four, upstream).astype(
        jnp.bfloat16
    )
    held_back = lax.optimization_barrier(
        (
            query_weight,
            key_weight,
            value_weight,
            output_weight,
            gate_weight,
            up_weight,
            down_weight,
            branch_two_grad,
        )
    )
    query_full, key_full, value_full, output_full, gate_full, up_full, down_full = (
        lax.all_gather(held_back[0], "fsdp", axis=0, tiled=True),
        lax.all_gather(held_back[1], "fsdp", axis=0, tiled=True),
        lax.all_gather(held_back[2], "fsdp", axis=0, tiled=True),
        lax.all_gather(held_back[3], "fsdp", axis=0, tiled=True),
        lax.all_gather(held_back[4], "fsdp", axis=0, tiled=True),
        lax.all_gather(held_back[5], "fsdp", axis=0, tiled=True),
        lax.all_gather(held_back[6], "fsdp", axis=0, tiled=True),
    )
    branch_two_grad = held_back[7]
    feed_grad_rows = lax.all_gather(branch_two_grad, "tp", axis=0, tiled=True)
    hidden_grad = jnp.dot(feed_grad_rows, down_full, preferred_element_type=jnp.float32)
    unused_out, pullback = jax.vjp(gelu_product, gate_value, up_value)
    gate_grad, up_grad = pullback(hidden_grad)
    gate_up_grad = jnp.concatenate(
        [gate_grad.astype(jnp.bfloat16), up_grad.astype(jnp.bfloat16)], axis=1
    )
    feed_split = gate_full.shape[1]
    shard_rows = query_weight.shape[0]
    left_rows = feed_input
    feed_weight_grads = lax.psum_scatter(
        jnp.concatenate(
            [contract_first(left_rows, gate_up_grad), contract_first(feed_grad_rows, hidden)],
            axis=1,
        ),
        "fsdp",
        scatter_dimension=0,
        tiled=True,
    )
    row_piece = gate_up_grad
    normed_three_grad = lax.psum_scatter(
        contract_last(row_piece[:, :feed_split], gate_full)
        + contract_last(row_piece[:, feed_split:], up_full),
        "tp",
        scatter_dimension=0,
        tiled=True,
    )
    gain_three_grad = jnp.sum(normed_three_grad * unit_three, axis=0)
    middle_grad = upstream + norm_backward(unit_three, inverse_three, gain_three, normed_three_grad)
    gain_two_grad = jnp.sum(middle_grad * unit_two, axis=0)
    branch_one_grad = norm_backward(unit_two, inverse_two, gain_two, middle_grad).astype(
        jnp.bfloat16
    )
    attention_grad_rows = lax.all_gather(branch_one_grad, "tp", axis=0, tiled=True)
    mixed_grad = jnp.dot(
        attention_grad_rows, output_full, preferred_element_type=jnp.float32
    ).astype(jnp.bfloat16)
    mixed_grad = mixed_grad.reshape(grouped_rows, kv_local, repeat_heads, HEAD_SIZE)
    capped_again, tanh_again = masked_scores(rotated_query, rotated_key, visible_mask)
    probs_again = jnp.exp(capped_again - log_total)
    value_grad = jnp.einsum(
        "grqk,qgrd->kgd",
        probs_again.astype(jnp.bfloat16),
        mixed_grad,
        preferred_element_type=jnp.float32,
    )
    probs_grad = jnp.einsum(
        "qgrd,kgd->grqk", mixed_grad, value_reduced, preferred_element_type=jnp.float32
    )
    score_grad = probs_again * (
        probs_grad - jnp.sum(probs_again * probs_grad, axis=-1, keepdims=True)
    )
    raw_grad = (score_grad * (1.0 - tanh_again * tanh_again) * HEAD_SIZE ** (-0.5)).astype(
        jnp.bfloat16
    )
    query_grad = jnp.einsum(
        "grqk,kgd->qgrd", raw_grad, rotated_key, preferred_element_type=jnp.float32
    )
    key_grad = jnp.einsum(
        "grqk,qgrd->kgd", raw_grad, rotated_query, preferred_element_type=jnp.float32
    )
    query_grad = unrotate(
        query_grad.reshape(grouped_rows, heads_local, HEAD_SIZE), cosine_lookup, sine_lookup
    )
    key_grad = unrotate(key_grad, cosine_lookup, sine_lookup)
    projected_grad = jnp.concatenate(
        [
            query_grad.reshape(grouped_rows, heads_local * HEAD_SIZE).astype(jnp.bfloat16),
            key_grad.reshape(grouped_rows, kv_local * HEAD_SIZE).astype(jnp.bfloat16),
            value_grad.reshape(grouped_rows, kv_local * HEAD_SIZE).astype(jnp.bfloat16),
        ],
        axis=1,
    )
    query_width = query_full.shape[1]
    key_width = key_full.shape[1]
    left_rows = normed
    attention_weight_grads = lax.psum_scatter(
        jnp.concatenate(
            [
                contract_first(left_rows, projected_grad),
                contract_first(attention_grad_rows, attended),
            ],
            axis=1,
        ),
        "fsdp",
        scatter_dimension=0,
        tiled=True,
    )
    row_piece = projected_grad
    total = contract_last(row_piece[:, :query_width], query_full)
    total = total + contract_last(row_piece[:, query_width : query_width + key_width], key_full)
    normed_one_grad = lax.psum_scatter(
        (total + contract_last(row_piece[:, query_width + key_width :], value_full)).astype(
            jnp.bfloat16
        ),
        "tp",
        scatter_dimension=0,
        tiled=True,
    ).astype(jnp.float32)
    gain_one_grad = jnp.sum(normed_one_grad * unit_one, axis=0)
    input_gradient = middle_grad + norm_backward(unit_one, inverse_one, gain_one, normed_one_grad)
    gain_sums = lax.psum(
        (gain_one_grad, gain_two_grad, gain_three_grad, gain_four_grad), ("fsdp", "tp")
    )
    offset = lax.axis_index("fsdp") * shard_rows
    gain_shards = [
        lax.dynamic_slice_in_dim(total_sum, offset, shard_rows) for total_sum in gain_sums
    ]
    value_start = query_width + key_width
    output_start = value_start + key_width
    return (
        block_output,
        input_gradient,
        gain_shards[0],
        gain_shards[1],
        gain_shards[2],
        gain_shards[3],
        attention_weight_grads[:, :query_width],
        attention_weight_grads[:, query_width:value_start],
        attention_weight_grads[:, value_start:output_start],
        attention_weight_grads[:, output_start:],
        feed_weight_grads[:, :feed_split],
        feed_weight_grads[:, feed_split : 2 * feed_split],
        feed_weight_grads[:, 2 * feed_split :],
    )


def solution(mesh):
    placed = (
        P(("fsdp", "tp"), None),
        P("fsdp", None),
        P("fsdp"),
        P("fsdp"),
        P("fsdp"),
        P("fsdp"),
        P("fsdp", "tp"),
        P("fsdp", "tp"),
        P("fsdp", "tp"),
        P("fsdp", "tp"),
        P("fsdp", "tp"),
        P("fsdp", "tp"),
        P("fsdp", "tp"),
        P(("fsdp", "tp"), None),
    )
    return jax.shard_map(
        shards,
        mesh=mesh,
        in_specs=placed,
        out_specs=(
            P(("fsdp", "tp"), None),
            P(("fsdp", "tp"), None),
            P("fsdp"),
            P("fsdp"),
            P("fsdp"),
            P("fsdp"),
            P("fsdp", "tp"),
            P("fsdp", "tp"),
            P("fsdp", "tp"),
            P("fsdp", "tp"),
            P("fsdp", "tp"),
            P("fsdp", "tp"),
            P("fsdp", "tp"),
        ),
        check_vma=False,
    )
```

profile of v0, /device:TPU:0, one launch (start us, length us, event | category | flops | bytes accessed | tf_op | source)
XLA Modules:
  0.0 2708.5 jit_solution(12363852051479386329)
XLA Ops:
  15.4 63.9 %all-reduce.5 = (bf16[2304]{0:T(1024)(128)(2,1)S(1)}, bf16[2304]{0:T(1024)(128)(2,1)S(1)}, bf16[2304]{0:T(1024)(128)(2,1)S(1)}, bf16[2304]{0:T(1024)(128)(2,1)S(1)}) all-reduce(bf16[2304]{0:T(1024)(128)(2,1)S(1)} %dynamic-update-slice, bf16[2304]{0:T(1024)(128)(2,1)S(1)} %dynamic-update-slice.1, ...), channel_id=1, replica_groups=mesh['fsdp'=16,'tp'=2] {'fsdp'}, use_global_device_ids=true, to_apply=%add | all-reduce | flops 9216 | bytes 36864
  101.6 51.6 %all-gather.19.cloned.1.call-done = bf16[2304,1024]{1,0:T(8,128)(2,1)} async-done(((bf16[144,1024]{1,0:T(8,128)(2,1)}), bf16[2304,1024]{1,0:T(8,128)(2,1)}) %all-gather.19.cloned.1.call-update) | async-done | bytes 4718608 | tf_op jit(solution)/shard_map/all_gather | solution.py:122
  159.3 47.7 %all-gather.21.cloned.1.call-done = bf16[2304,1024]{1,0:T(8,128)(2,1)} async-done(((bf16[144,1024]{1,0:T(8,128)(2,1)}), bf16[2304,1024]{1,0:T(8,128)(2,1)}) %all-gather.21.cloned.1.call-update) | async-done | bytes 4718608 | tf_op jit(solution)/shard_map/all_gather | solution.py:125
  214.4 24.9 reduce-scatter.9.cloned.1.call-done
  255.1 95.7 %all-gather.23.cloned.1.call-done = bf16[2304,4608]{1,0:T(8,128)(2,1)} async-done(((bf16[144,4608]{1,0:T(8,128)(2,1)}), bf16[2304,4608]{1,0:T(8,128)(2,1)}) %all-gather.23.cloned.1.call-update) | async-done | bytes 21233680 | tf_op jit(solution)/shard_map/all_gather | solution.py:130
  362.2 100.3 %all-gather.25.cloned.1.call-done = bf16[2304,4608]{1,0:T(8,128)(2,1)} async-done(((bf16[144,4608]{1,0:T(8,128)(2,1)}), bf16[2304,4608]{1,0:T(8,128)(2,1)}) %all-gather.25.cloned.1.call-update) | async-done | bytes 21233680 | tf_op jit(solution)/shard_map/all_gather | solution.py:131
  477.2 96.9 %all-gather.27.cloned.1.call-done = bf16[2304,4608]{1,0:T(8,128)(2,1)} async-done(((bf16[144,4608]{1,0:T(8,128)(2,1)}), bf16[2304,4608]{1,0:T(8,128)(2,1)}) %all-gather.27.cloned.1.call-update) | async-done | bytes 21233680 | tf_op jit(solution)/shard_map/all_gather | solution.py:132
  586.8 28.4 %reduce-scatter.11.cloned.1.call-done = f32[96,2304]{1,0:T(8,128)} async-done(((f32[192,2304]{1,0:T(8,128)}), f32[96,2304]{1,0:T(8,128)}) %reduce-scatter.11.cloned.1.call-update) | async-done | bytes 884752 | tf_op jit(solution)/shard_map/reduce_scatter | solution.py:187
  635.1 95.9 %all-gather.29.cloned.1.call-done = bf16[2304,4608]{1,0:T(8,128)(2,1)} async-done(((bf16[144,4608]{1,0:T(8,128)(2,1)}), bf16[2304,4608]{1,0:T(8,128)(2,1)}) %all-gather.29.cloned.1.call-update) | async-done | bytes 21233680 | tf_op jit(solution)/shard_map/all_gather | solution.py:216
  745.2 97.4 %all-gather.31.cloned.1.call-done = bf16[2304,4608]{1,0:T(8,128)(2,1)} async-done(((bf16[144,4608]{1,0:T(8,128)(2,1)}), bf16[2304,4608]{1,0:T(8,128)(2,1)}) %all-gather.31.cloned.1.call-update) | async-done | bytes 21233680 | tf_op jit(solution)/shard_map/all_gather | solution.py:214
  855.2 98.8 %all-gather.33.cloned.1.call-done = bf16[2304,4608]{1,0:T(8,128)(2,1)} async-done(((bf16[144,4608]{1,0:T(8,128)(2,1)}), bf16[2304,4608]{1,0:T(8,128)(2,1)}) %all-gather.33.cloned.1.call-update) | async-done | bytes 21233680 | tf_op jit(solution)/shard_map/all_gather | solution.py:215
  969.6 26.1 reduce-scatter.13.cloned.1.call-done
  1013.4 37.5 %all-gather.35.cloned.1.call-done = bf16[2304,1024]{1,0:T(8,128)(2,1)} async-done(((bf16[144,1024]{1,0:T(8,128)(2,1)}), bf16[2304,1024]{1,0:T(8,128)(2,1)}) %all-gather.35.cloned.1.call-update) | async-done | bytes 4718608 | tf_op jit(solution)/shard_map/all_gather | solution.py:213
  1067.1 37.7 %all-gather.37.cloned.1.call-done = bf16[2304,1024]{1,0:T(8,128)(2,1)} async-done(((bf16[144,1024]{1,0:T(8,128)(2,1)}), bf16[2304,1024]{1,0:T(8,128)(2,1)}) %all-gather.37.cloned.1.call-update) | async-done | bytes 4718608 | tf_op jit(solution)/shard_map/all_gather | solution.py:210
  1110.1 37.7 %all-gather.39.cloned.1.call-done = bf16[2304,512]{1,0:T(8,128)(2,1)} async-done(((bf16[144,512]{1,0:T(8,128)(2,1)}), bf16[2304,512]{1,0:T(8,128)(2,1)}) %all-gather.39.cloned.1.call-update) | async-done | bytes 2359312 | tf_op jit(solution)/shard_map/all_gather | solution.py:211
  1164.1 26.9 all-gather.41.cloned.1.call-done
  1194.6 18.8 pad_maximum_fusion.1
  1213.4 27.7 %copy.111 = f32[2304,3072]{1,0:T(8,128)} copy(f32[2304,3072]{0,1:T(8,128)} %pad_maximum_fusion.1) | data formatting | bytes 56623104
  1242.3 27.8 %fusion.115 = f32[2304,4608]{1,0:T(8,128)} fusion(bf16[192,2304]{1,0:T(8,128)(2,1)S(1)} %copy-done.6, bf16[192,4608]{1,0:T(8,128)(2,1)} %get-tuple-element.129), kind=kOutput, calls=%fused_computation.171 | convolution fusion | flops 4076863488 | bytes 45121536 | tf_op jit(solution)/shard_map/dot_general | solution.py:20
  1270.1 32.5 %fusion.9 = f32[2304,9216]{1,0:T(8,128)} fusion(bf16[192,2304]{1,0:T(8,128)(2,1)S(1)} %copy-done.9, bf16[192,4608]{1,0:T(8,128)(2,1)S(1)} %copy-done.17, bf16[192,4608]{1,0:T(8,128)(2,1)S(1)} %copy-done.18), kind=kOutput, calls=%fused_computation.16 | convolution fusion | flops 8160804864 | bytes 89358336 | tf_op jit(solution)/shard_map/dot_general | solution.py:20
  1302.7 85.6 %pad_maximum_fusion = f32[2304,13824]{1,0:T(8,128)} fusion(f32[2304,4608]{1,0:T(8,128)} %fusion.115, f32[2304,9216]{1,0:T(8,128)} %fusion.9), kind=kLoop, calls=%fused_computation.1 | loop fusion | flops 31850496 | bytes 254803968 | tf_op jit(solution)/shard_map/concatenate | solution.py:230
  1390.7 40.4 %all-reduce.4 = (f32[2304]{0:T(1024)S(1)}, f32[2304]{0:T(1024)S(1)}, f32[2304]{0:T(1024)S(1)}, f32[2304]{0:T(1024)S(1)}) all-reduce(f32[2304]{0:T(1024)S(1)} %get-tuple-element.87, f32[2304]{0:T(1024)S(1)} %copy-done.40, f32[2304]{0:T(1024)S(1)} %copy-done.39, f32[2304]{0:T(1024)S(1)} %copy-done.38), channel_id=1, replica_groups=mesh['fsdp'=16,'tp'=2] {'fsdp','tp'}, use_global_device_ids=true, to_apply=%region_19.20 | all-reduce | flops 9216 | bytes 73728 | tf_op jit(solution)/shard_map/psum | solution.py:320
  1436.0 76.9 %reduce-scatter.19.cloned.1.call-done = f32[144,3072]{1,0:T(8,128)} async-done(((f32[2304,3072]{1,0:T(8,128)}), f32[144,3072]{1,0:T(8,128)}) %reduce-scatter.19.cloned.1.call-update) | async-done | bytes 1769488
  1517.2 1177.5 %reduce-scatter.17.cloned.1.call-done = f32[144,13824]{1,0:T(8,128)} async-done(((f32[2304,13824]{1,0:T(8,128)}), f32[144,13824]{1,0:T(8,128)}) %reduce-scatter.17.cloned.1.call-update) | async-done | bytes 7962640 | tf_op jit(solution)/shard_map/reduce_scatter | solution.py:229
  (236 shorter events, 237.8 us)
Async XLA Ops:
  7.2 85.1 %copy-start.47 = (s32[1,9]{1,0:T(1,128)S(1)}, s32[1,9]{1,0:T(1,128)}, u32[]{:S(2)}) copy-start(s32[1,9]{1,0:T(1,128)} %param.15) | copy-start | bytes 112
  7.2 85.8 %all-gather.17.cloned.1.call-start = ((), (), s32[]{:S(2)}) async-start(), calls=%async_computation.7 | async-start | bytes 2506752 | tf_op jit(solution)/shard_map/all_gather | solution.py:123
  7.9 91.1 %all-gather.15.cloned.1.call-start = ((), (), s32[]{:S(2)}) async-start(), calls=%async_computation.6 | async-start | bytes 2506752 | tf_op jit(solution)/shard_map/all_gather | solution.py:124
  8.7 144.5 %all-gather.19.cloned.1.call-start = ((), (), s32[]{:S(2)}) async-start(), calls=%async_computation.8 | async-start | bytes 5013504 | tf_op jit(solution)/shard_map/all_gather | solution.py:122
  9.4 197.6 %all-gather.21.cloned.1.call-start = ((), (), s32[]{:S(2)}) async-start(), calls=%async_computation.9 | async-start | bytes 5013504 | tf_op jit(solution)/shard_map/all_gather | solution.py:125
  10.0 229.3 %reduce-scatter.9.cloned.1.call-start = ((), (), s32[]{:S(2)}) async-start(), calls=%async_computation.10 | async-start | bytes 2654208 | tf_op jit(solution)/shard_map/reduce_scatter | solution.py:175
  92.5 65.4 %copy-start.29 = (pred[192,192]{0,1:T(8,128)(4,1)}, pred[192,192]{0,1:T(8,128)(4,1)S(1)}, u32[]{:S(2)}) copy-start(pred[192,192]{0,1:T(8,128)(4,1)S(1)} %fusion.77) | copy-start | bytes 110596
  212.3 138.5 %all-gather.23.cloned.1.call-start = ((), (), s32[]{:S(2)}) async-start(), calls=%async_computation.11 | async-start | bytes 22560768 | tf_op jit(solution)/shard_map/all_gather | solution.py:130
  212.8 249.6 %all-gather.25.cloned.1.call-start = ((), (), s32[]{:S(2)}) async-start(), calls=%async_computation.12 | async-start | bytes 22560768 | tf_op jit(solution)/shard_map/all_gather | solution.py:131
  213.6 360.4 %all-gather.27.cloned.1.call-start = ((), (), s32[]{:S(2)}) async-start(), calls=%async_computation.13 | async-start | bytes 22560768 | tf_op jit(solution)/shard_map/all_gather | solution.py:132
  214.3 400.8 %reduce-scatter.11.cloned.1.call-start = ((), (), s32[]{:S(2)}) async-start(), calls=%async_computation.14 | async-start | bytes 2654208 | tf_op jit(solution)/shard_map/reduce_scatter | solution.py:187
  255.1 207.4 %copy-start.8 = (bf16[192,2304]{1,0:T(8,128)(2,1)}, bf16[192,2304]{1,0:T(8,128)(2,1)S(1)}, u32[]{:S(2)}) copy-start(bf16[192,2304]{1,0:T(8,128)(2,1)S(1)} %all_gather.74) | copy-start | bytes 2654212
  586.7 144.3 %all-gather.29.cloned.1.call-start = ((), (), s32[]{:S(2)}) async-start(), calls=%async_computation.15 | async-start | bytes 22560768 | tf_op jit(solution)/shard_map/all_gather | solution.py:216
  620.8 221.8 %all-gather.31.cloned.1.call-start = ((), (), s32[]{:S(2)}) async-start(), calls=%async_computation.16 | async-start | bytes 22560768 | tf_op jit(solution)/shard_map/all_gather | solution.py:214
  621.5 332.5 %all-gather.33.cloned.1.call-start = ((), (), s32[]{:S(2)}) async-start(), calls=%async_computation.17 | async-start | bytes 22560768 | tf_op jit(solution)/shard_map/all_gather | solution.py:215
  622.1 373.6 %reduce-scatter.13.cloned.1.call-start = ((), (), s32[]{:S(2)}) async-start(), calls=%async_computation.18 | async-start | bytes 2654208 | tf_op jit(solution)/shard_map/reduce_scatter | solution.py:239
  635.1 110.1 %copy-start.5 = (bf16[192,2304]{1,0:T(8,128)(2,1)}, bf16[192,2304]{1,0:T(8,128)(2,1)S(1)}, u32[]{:S(2)}) copy-start(bf16[192,2304]{1,0:T(8,128)(2,1)S(1)} %all_gather.79) | copy-start | bytes 2654212
  967.2 83.7 %all-gather.35.cloned.1.call-start = ((), (), s32[]{:S(2)}) async-start(), calls=%async_computation.19 | async-start | bytes 5013504 | tf_op jit(solution)/shard_map/all_gather | solution.py:213
  967.8 137.0 %all-gather.37.cloned.1.call-start = ((), (), s32[]{:S(2)}) async-start(), calls=%async_computation.20 | async-start | bytes 5013504 | tf_op jit(solution)/shard_map/all_gather | solution.py:210
  968.4 179.4 %all-gather.39.cloned.1.call-start = ((), (), s32[]{:S(2)}) async-start(), calls=%async_computation.21 | async-start | bytes 2506752 | tf_op jit(solution)/shard_map/all_gather | solution.py:211
  969.0 222.0 %all-gather.41.cloned.1.call-start = ((), (), s32[]{:S(2)}) async-start(), calls=%async_computation.22 | async-start | bytes 2506752 | tf_op jit(solution)/shard_map/all_gather | solution.py:212
  969.6 418.8 %reduce-scatter.15.cloned.1.call-start = ((), (), s32[]{:S(2)}) async-start(), calls=%async_computation.23 | async-start | bytes 1327104 | tf_op jit(solution)/shard_map/reduce_scatter | solution.py:310
  1194.6 318.4 %reduce-scatter.19.cloned.1.call-start = ((), (), s32[]{:S(2)}) async-start(), calls=%async_computation.25 | async-start | bytes 30081024
  1241.2 1453.5 %reduce-scatter.17.cloned.1.call-start = ((), (), s32[]{:S(2)}) async-start(), calls=%async_computation.24 | async-start | bytes 135364608 | tf_op jit(solution)/shard_map/reduce_scatter | solution.py:229
  (44 other events, 1063.7 us)
Sparse Core Ops, SparseCore 0:
  10.3 45.2 all-gather.16
  57.8 41.0 all-gather.14
  101.3 51.8 all-gather.18
  155.3 51.6 all-gather.20
  212.4 26.8 reduce-scatter.8
  240.7 110.0 all-gather.22
  352.4 109.9 all-gather.24
  464.0 109.9 all-gather.26
  586.8 28.2 reduce-scatter.10
  620.9 109.9 all-gather.28
  732.6 109.9 all-gather.30
  844.0 109.9 all-gather.32
  967.3 28.2 reduce-scatter.12
  997.8 53.1 all-gather.34
  1053.1 51.6 all-gather.36
  1106.9 40.8 all-gather.38
  1150.0 41.0 all-gather.40
  1194.7 17.3 reduce-scatter.14
  1241.3 271.5 reduce-scatter.18
  1517.0 1177.6 reduce-scatter.16
where the time goes:
time: 2720 us; the launch traced here: 2710 us
  waiting for transfers between devices  2170 us (80%)
  matrix products  189 us (7%)
  blocking collectives  151 us (6%)
  other arithmetic  127 us (5%)
  local copies, waits for them, and re-layouts  54.3 us (2%)
    reduce_scatter x1, waiting for transfers between devices, shards(): lax.psum_scatter(jnp.concatenate([contract_first(left_rows, gate_up_grad)...  1180 us
    all_gather x1, waiting for transfers between devices, shards(): lax.all_gather(up_weight, 'fsdp', axis=0, tiled=True)  100 us
    all_gather x1, waiting for transfers between devices, shards(): lax.all_gather(held_back[5], 'fsdp', axis=0, tiled=True)  98.8 us
    all_gather x1, waiting for transfers between devices, shards(): lax.all_gather(held_back[4], 'fsdp', axis=0, tiled=True)  97.4 us
    all_gather x1, waiting for transfers between devices, shards(): lax.all_gather(down_weight, 'fsdp', axis=0, tiled=True)  96.9 us
    all_gather x1, waiting for transfers between devices, shards(): lax.all_gather(held_back[6], 'fsdp', axis=0, tiled=True)  95.9 us
    all_gather x1, waiting for transfers between devices, shards(): lax.all_gather(gate_weight, 'fsdp', axis=0, tiled=True)  95.7 us
    concatenate x1, other arithmetic, shards(): jnp.concatenate([contract_first(left_rows, gate_up_grad), contract_first(...  85.6 us
  transfers between devices with their start and end apart: 20, of which 18 were waited for; matrix products, arithmetic and copies ran while one was open for 12% of the time, Pallas kernels for 0%

commit v1 on v0

--- a/solution.py
+++ b/solution.py
@@ -8,6 +8,18 @@
 EPSILON = 1e-06
 SOFTCAP = 50.0
 NEGATIVE = -1e30
+
+
+def collect(x, axis, dim):
+    ways, here = (lax.axis_size(axis), lax.axis_index(axis))
+    grown, reach = (x, 1)
+    while reach < ways:
+        theirs = lax.ppermute(grown, axis, [(d, d ^ reach) for d in range(ways)])
+        mine_first = jnp.concatenate([grown, theirs], axis=dim)
+        theirs_first = jnp.concatenate([theirs, grown], axis=dim)
+        grown = jnp.where(here & reach == 0, mine_first, theirs_first)
+        reach = 2 * reach
+    return grown
 
 
 def contract_last(left_rows, right_rows):
@@ -213,7 +225,7 @@
         lax.all_gather(held_back[3], "fsdp", axis=0, tiled=True),
         lax.all_gather(held_back[4], "fsdp", axis=0, tiled=True),
         lax.all_gather(held_back[5], "fsdp", axis=0, tiled=True),
-        lax.all_gather(held_back[6], "fsdp", axis=0, tiled=True),
+        collect(held_back[6], "fsdp", 0),
     )
     branch_two_grad = held_back[7]
     feed_grad_rows = lax.all_gather(branch_two_grad, "tp", axis=0, tiled=True)

time: 2720 us -> 3230 us (1.19)
  waiting for transfers between devices: 2170 us -> 2650 us
    ppermute x0 -> x4, waiting for transfers between devices: none -> 778 us  [collect(): theirs = lax.ppermute(grown, axis, [(d, d ^ reach) for d in range(ways)])]
    all_gather x1, waiting for transfers between devices: 98.8 us -> 0.01 us  [shards(): lax.all_gather(held_back[5], 'fsdp', axis=0, tiled=True)]
    all_gather x1, waiting for transfers between devices: 97.4 us -> 0.01 us  [shards(): lax.all_gather(held_back[4], 'fsdp', axis=0, tiled=True)]
    all_gather x1 -> x0, waiting for transfers between devices: 95.9 us -> none  [shards(): lax.all_gather(held_back[6], 'fsdp', axis=0, tiled=True)]
    unnamed x21 -> x20, waiting for transfers between devices: 84.9 us -> 85.7 us
  transfers between devices with their start and end apart: 20 -> 23, of which waited for: 18 -> 19; matrix products, arithmetic and copies ran while one was open for 12% -> 11% of each run, Pallas kernels for 0% -> 0%
where the time goes in v1:
time: 3230 us; the launch traced here: 3220 us
  waiting for transfers between devices  2650 us (82%)
  matrix products  195 us (6%)
  blocking collectives  150 us (5%)
  other arithmetic  149 us (5%)
  local copies, waits for them, and re-layouts  53.5 us (2%)
    reduce_scatter x1, waiting for transfers between devices, shards(): lax.psum_scatter(jnp.concatenate([contract_first(left_rows, gate_up_grad)...  1180 us
    ppermute x4, waiting for transfers between devices, collect(): theirs = lax.ppermute(grown, axis, [(d, d ^ reach) for d in range(ways)])  778 us
    all_gather x1, waiting for transfers between devices, shards(): lax.all_gather(up_weight, 'fsdp', axis=0, tiled=True)  100 us
    all_gather x1, waiting for transfers between devices, shards(): lax.all_gather(down_weight, 'fsdp', axis=0, tiled=True)  96.9 us
    all_gather x1, waiting for transfers between devices, shards(): lax.all_gather(gate_weight, 'fsdp', axis=0, tiled=True)  95.9 us
    unnamed x20, waiting for transfers between devices  85.7 us
    concatenate x1, other arithmetic, shards(): jnp.concatenate([contract_first(left_rows, gate_up_grad), contract_first(...  85.1 us
    dot_general x4, matrix products, contract_first(): lax.dot_general(left_rows, right_rows, (((0,), (0,)), ((), ())), preferre...  73.4 us
  transfers between devices with their start and end apart: 23, of which 19 were waited for; matrix products, arithmetic and copies ran while one was open for 11% of the time, Pallas kernels for 0%

profile of v1, /device:TPU:0, one launch (start us, length us, event | category | flops | bytes accessed | tf_op | source)
XLA Modules:
  0.0 3224.3 jit_solution(6757925401088185730)
XLA Ops:
  15.4 63.9 %all-reduce.5 = (bf16[2304]{0:T(1024)(128)(2,1)S(1)}, bf16[2304]{0:T(1024)(128)(2,1)S(1)}, bf16[2304]{0:T(1024)(128)(2,1)S(1)}, bf16[2304]{0:T(1024)(128)(2,1)S(1)}) all-reduce(bf16[2304]{0:T(1024)(128)(2,1)S(1)} %dynamic-update-slice, bf16[2304]{0:T(1024)(128)(2,1)S(1)} %dynamic-update-slice.1, ...), channel_id=1, replica_groups=mesh['fsdp'=16,'tp'=2] {'fsdp'}, use_global_device_ids=true, to_apply=%add | all-reduce | flops 9216 | bytes 36864
  101.6 51.6 %all-gather.18.cloned.1.call-done = bf16[2304,1024]{1,0:T(8,128)(2,1)} async-done(((bf16[144,1024]{1,0:T(8,128)(2,1)}), bf16[2304,1024]{1,0:T(8,128)(2,1)}) %all-gather.18.cloned.1.call-update) | async-done | bytes 4718608 | tf_op jit(solution)/shard_map/all_gather | solution.py:134
  159.3 47.7 %all-gather.20.cloned.1.call-done = bf16[2304,1024]{1,0:T(8,128)(2,1)} async-done(((bf16[144,1024]{1,0:T(8,128)(2,1)}), bf16[2304,1024]{1,0:T(8,128)(2,1)}) %all-gather.20.cloned.1.call-update) | async-done | bytes 4718608 | tf_op jit(solution)/shard_map/all_gather | solution.py:137
  214.4 24.9 reduce-scatter.9.cloned.1.call-done
  254.9 95.9 %all-gather.22.cloned.1.call-done = bf16[2304,4608]{1,0:T(8,128)(2,1)} async-done(((bf16[144,4608]{1,0:T(8,128)(2,1)}), bf16[2304,4608]{1,0:T(8,128)(2,1)}) %all-gather.22.cloned.1.call-update) | async-done | bytes 21233680 | tf_op jit(solution)/shard_map/all_gather | solution.py:142
  362.2 100.3 %all-gather.24.cloned.1.call-done = bf16[2304,4608]{1,0:T(8,128)(2,1)} async-done(((bf16[144,4608]{1,0:T(8,128)(2,1)}), bf16[2304,4608]{1,0:T(8,128)(2,1)}) %all-gather.24.cloned.1.call-update) | async-done | bytes 21233680 | tf_op jit(solution)/shard_map/all_gather | solution.py:143
  477.2 96.9 %all-gather.26.cloned.1.call-done = bf16[2304,4608]{1,0:T(8,128)(2,1)} async-done(((bf16[144,4608]{1,0:T(8,128)(2,1)}), bf16[2304,4608]{1,0:T(8,128)(2,1)}) %all-gather.26.cloned.1.call-update) | async-done | bytes 21233680 | tf_op jit(solution)/shard_map/all_gather | solution.py:144
  586.8 28.4 reduce-scatter.11.cloned.1.call-done
  629.8 115.7 %collective-permute-done.1 = bf16[288,4608]{1,0:T(8,128)(2,1)} collective-permute-done((bf16[288,4608]{1,0:T(8,128)(2,1)S(1)}, bf16[288,4608]{1,0:T(8,128)(2,1)}, u32[]{:S(2)}, u32[]{:S(2)}) %collective-permute-start.1) | collective-permute-done | bytes 2654240 | tf_op jit(solution)/shard_map/ppermute | solution.py:17
  751.8 215.7 %collective-permute-done.2 = bf16[576,4608]{1,0:T(8,128)(2,1)} collective-permute-done((bf16[576,4608]{1,0:T(8,128)(2,1)}, bf16[576,4608]{1,0:T(8,128)(2,1)}, u32[]{:S(2)}, u32[]{:S(2)}) %collective-permute-start.2) | collective-permute-done | bytes 5308448 | tf_op jit(solution)/shard_map/ppermute | solution.py:17
  995.4 443.8 %collective-permute-done.3 = bf16[1152,4608]{1,0:T(8,128)(2,1)} collective-permute-done((bf16[1152,4608]{1,0:T(8,128)(2,1)}, bf16[1152,4608]{1,0:T(8,128)(2,1)}, u32[]{:S(2)}, u32[]{:S(2)}) %collective-permute-start.3) | collective-permute-done | bytes 10616864 | tf_op jit(solution)/shard_map/ppermute | solution.py:17
  1439.3 19.5 multiply_convert_fusion
  1487.7 23.9 reduce-scatter.13.cloned.1.call-done
  1529.6 37.4 %all-gather.32.cloned.1.call-done = bf16[2304,1024]{1,0:T(8,128)(2,1)} async-done(((bf16[144,1024]{1,0:T(8,128)(2,1)}), bf16[2304,1024]{1,0:T(8,128)(2,1)}) %all-gather.32.cloned.1.call-update) | async-done | bytes 4718608 | tf_op jit(solution)/shard_map/all_gather | solution.py:225
  1583.0 37.9 %all-gather.34.cloned.1.call-done = bf16[2304,1024]{1,0:T(8,128)(2,1)} async-done(((bf16[144,1024]{1,0:T(8,128)(2,1)}), bf16[2304,1024]{1,0:T(8,128)(2,1)}) %all-gather.34.cloned.1.call-update) | async-done | bytes 4718608 | tf_op jit(solution)/shard_map/all_gather | solution.py:222
  1626.1 37.8 %all-gather.36.cloned.1.call-done = bf16[2304,512]{1,0:T(8,128)(2,1)} async-done(((bf16[144,512]{1,0:T(8,128)(2,1)}), bf16[2304,512]{1,0:T(8,128)(2,1)}) %all-gather.36.cloned.1.call-update) | async-done | bytes 2359312 | tf_op jit(solution)/shard_map/all_gather | solution.py:223
  1680.2 26.9 all-gather.38.cloned.1.call-done
  1729.6 27.7 copy.111
  1757.6 27.1 fusion.123
  1784.7 33.3 %fusion.16 = f32[2304,9216]{1,0:T(8,128)} fusion(bf16[192,2304]{1,0:T(8,128)(2,1)S(1)} %copy-done.11, bf16[192,4608]{1,0:T(8,128)(2,1)S(1)} %copy-done.21, bf16[192,4608]{1,0:T(8,128)(2,1)S(1)} %copy-done.22), kind=kOutput, calls=%fused_computation.26 | convolution fusion | flops 8160804864 | bytes 89358336 | tf_op jit(solution)/shard_map/dot_general | solution.py:32
  1817.9 85.1 %pad_maximum_fusion = f32[2304,13824]{1,0:T(8,128)} fusion(f32[2304,4608]{1,0:T(8,128)} %fusion.123, f32[2304,9216]{1,0:T(8,128)} %fusion.16), kind=kLoop, calls=%fused_computation.1 | loop fusion | flops 31850496 | bytes 254803968 | tf_op jit(solution)/shard_map/concatenate | solution.py:242
  1905.5 40.6 %all-reduce.4 = (f32[2304]{0:T(1024)S(1)}, f32[2304]{0:T(1024)S(1)}, f32[2304]{0:T(1024)S(1)}, f32[2304]{0:T(1024)S(1)}) all-reduce(f32[2304]{0:T(1024)S(1)} %get-tuple-element.87, f32[2304]{0:T(1024)S(1)} %copy-done.44, f32[2304]{0:T(1024)S(1)} %copy-done.43, f32[2304]{0:T(1024)S(1)} %copy-done.42), channel_id=1, replica_groups=mesh['fsdp'=16,'tp'=2] {'fsdp','tp'}, use_global_device_ids=true, to_apply=%region_19.20 | all-reduce | flops 9216 | bytes 73728 | tf_op jit(solution)/shard_map/psum | solution.py:332
  1950.9 78.1 %reduce-scatter.19.cloned.1.call-done = f32[144,3072]{1,0:T(8,128)} async-done(((f32[2304,3072]{1,0:T(8,128)}), f32[144,3072]{1,0:T(8,128)}) %reduce-scatter.19.cloned.1.call-update) | async-done | bytes 1769488
  2033.3 1177.5 %reduce-scatter.17.cloned.1.call-done = f32[144,13824]{1,0:T(8,128)} async-done(((f32[2304,13824]{1,0:T(8,128)}), f32[144,13824]{1,0:T(8,128)}) %reduce-scatter.17.cloned.1.call-update) | async-done | bytes 7962640 | tf_op jit(solution)/shard_map/reduce_scatter | solution.py:241
  (252 shorter events, 271.1 us)
Async XLA Ops:
  7.2 85.8 %all-gather.16.cloned.1.call-start = ((), (), s32[]{:S(2)}) async-start(), calls=%async_computation.7 | async-start | bytes 2506752 | tf_op jit(solution)/shard_map/all_gather | solution.py:135
  7.9 91.1 %all-gather.14.cloned.1.call-start = ((), (), s32[]{:S(2)}) async-start(), calls=%async_computation.6 | async-start | bytes 2506752 | tf_op jit(solution)/shard_map/all_gather | solution.py:136
  8.7 144.5 %all-gather.18.cloned.1.call-start = ((), (), s32[]{:S(2)}) async-start(), calls=%async_computation.8 | async-start | bytes 5013504 | tf_op jit(solution)/shard_map/all_gather | solution.py:134
  9.4 197.6 %all-gather.20.cloned.1.call-start = ((), (), s32[]{:S(2)}) async-start(), calls=%async_computation.9 | async-start | bytes 5013504 | tf_op jit(solution)/shard_map/all_gather | solution.py:137
  10.0 229.3 %reduce-scatter.9.cloned.1.call-start = ((), (), s32[]{:S(2)}) async-start(), calls=%async_computation.10 | async-start | bytes 2654208 | tf_op jit(solution)/shard_map/reduce_scatter | solution.py:187
  212.3 138.5 %all-gather.22.cloned.1.call-start = ((), (), s32[]{:S(2)}) async-start(), calls=%async_computation.11 | async-start | bytes 22560768 | tf_op jit(solution)/shard_map/all_gather | solution.py:142
  212.9 249.6 %all-gather.24.cloned.1.call-start = ((), (), s32[]{:S(2)}) async-start(), calls=%async_computation.12 | async-start | bytes 22560768 | tf_op jit(solution)/shard_map/all_gather | solution.py:143
  213.6 360.4 %all-gather.26.cloned.1.call-start = ((), (), s32[]{:S(2)}) async-start(), calls=%async_computation.13 | async-start | bytes 22560768 | tf_op jit(solution)/shard_map/all_gather | solution.py:144
  214.4 400.8 %reduce-scatter.11.cloned.1.call-start = ((), (), s32[]{:S(2)}) async-start(), calls=%async_computation.14 | async-start | bytes 2654208 | tf_op jit(solution)/shard_map/reduce_scatter | solution.py:199
  586.7 872.1 %all-gather.28.cloned.1.call-start = ((), (), s32[]{:S(2)}) async-start(), calls=%async_computation.15 | async-start | bytes 22560768 | tf_op jit(solution)/shard_map/all_gather | solution.py:226
  621.1 850.9 %all-gather.30.cloned.1.call-start = ((), (), s32[]{:S(2)}) async-start(), calls=%async_computation.16 | async-start | bytes 22560768 | tf_op jit(solution)/shard_map/all_gather | solution.py:227
  621.8 889.8 %reduce-scatter.13.cloned.1.call-start = ((), (), s32[]{:S(2)}) async-start(), calls=%async_computation.17 | async-start | bytes 2654208 | tf_op jit(solution)/shard_map/reduce_scatter | solution.py:251
  621.9 3.3 collective-permute-start
  628.2 117.2 %collective-permute-start.1 = (bf16[288,4608]{1,0:T(8,128)(2,1)S(1)}, bf16[288,4608]{1,0:T(8,128)(2,1)}, u32[]{:S(2)}, u32[]{:S(2)}) collective-permute-start(bf16[288,4608]{1,0:T(8,128)(2,1)S(1)} %maximum_select_fusion.4), channel_id=1, source_target_pairs={{0,4},{2,6},{4,0},{6,2},{8,12},{10,14},{12,8},{14,10},{16,20},{18,... | collective-permute-start | bytes 7962632 | tf_op jit(solution)/shard_map/ppermute | solution.py:17
  751.8 215.7 %collective-permute-start.2 = (bf16[576,4608]{1,0:T(8,128)(2,1)}, bf16[576,4608]{1,0:T(8,128)(2,1)}, u32[]{:S(2)}, u32[]{:S(2)}) collective-permute-start(bf16[576,4608]{1,0:T(8,128)(2,1)} %maximum_select_fusion.3), channel_id=1, source_target_pairs={{0,8},{2,10},{4,12},{6,14},{8,0},{10,2},{12,4},{14,6},{16,24},{18,... | collective-permute-start | bytes 15925256 | tf_op jit(solution)/shard_map/ppermute | solution.py:17
  751.8 232.6 %copy-start.19 = (bf16[96,2304]{1,0:T(8,128)(2,1)S(1)}, bf16[96,2304]{1,0:T(8,128)(2,1)}, u32[]{:S(2)}) copy-start(bf16[96,2304]{1,0:T(8,128)(2,1)} %get-tuple-element.21) | copy-start | bytes 1327108
  980.2 459.1 %collective-permute-start.3 = (bf16[1152,4608]{1,0:T(8,128)(2,1)}, bf16[1152,4608]{1,0:T(8,128)(2,1)}, u32[]{:S(2)}, u32[]{:S(2)}) collective-permute-start(bf16[1152,4608]{1,0:T(8,128)(2,1)} %maximum_select_fusion.2), channel_id=1, source_target_pairs={{0,16},{2,18},{4,20},{6,22},{8,24},{10,26},{12,28},{14,30},{16,0},... | collective-permute-start | bytes 31850504 | tf_op jit(solution)/shard_map/ppermute | solution.py:17
  1485.1 81.9 %all-gather.32.cloned.1.call-start = ((), (), s32[]{:S(2)}) async-start(), calls=%async_computation.18 | async-start | bytes 5013504 | tf_op jit(solution)/shard_map/all_gather | solution.py:225
  1485.9 135.0 %all-gather.34.cloned.1.call-start = ((), (), s32[]{:S(2)}) async-start(), calls=%async_computation.19 | async-start | bytes 5013504 | tf_op jit(solution)/shard_map/all_gather | solution.py:222
  1486.5 177.5 %all-gather.36.cloned.1.call-start = ((), (), s32[]{:S(2)}) async-start(), calls=%async_computation.20 | async-start | bytes 2506752 | tf_op jit(solution)/shard_map/all_gather | solution.py:223
  1487.0 220.1 %all-gather.38.cloned.1.call-start = ((), (), s32[]{:S(2)}) async-start(), calls=%async_computation.21 | async-start | bytes 2506752 | tf_op jit(solution)/shard_map/all_gather | solution.py:224
  1487.6 415.5 %reduce-scatter.15.cloned.1.call-start = ((), (), s32[]{:S(2)}) async-start(), calls=%async_computation.22 | async-start | bytes 1327104 | tf_op jit(solution)/shard_map/reduce_scatter | solution.py:322
  1710.6 318.4 %reduce-scatter.19.cloned.1.call-start = ((), (), s32[]{:S(2)}) async-start(), calls=%async_computation.24 | async-start | bytes 30081024
  1757.3 1453.4 %reduce-scatter.17.cloned.1.call-start = ((), (), s32[]{:S(2)}) async-start(), calls=%async_computation.23 | async-start | bytes 135364608 | tf_op jit(solution)/shard_map/reduce_scatter | solution.py:241
  (51 other events, 1669.9 us)
Sparse Core Ops, SparseCore 0:
  10.3 45.2 all-gather.15
  57.8 41.0 all-gather.13
  101.3 51.8 all-gather.17
  155.3 51.6 all-gather.19
  212.4 26.8 reduce-scatter.8
  240.7 110.0 all-gather.21
  352.4 109.9 all-gather.23
  464.0 109.9 all-gather.25
  586.8 28.3 reduce-scatter.10
  621.2 179.7 all-gather.27
  802.6 191.8 all-gather.29
  1485.2 26.3 reduce-scatter.12
  1513.9 53.1 all-gather.31
  1569.2 51.6 all-gather.33
  1623.0 40.8 all-gather.35
  1666.0 41.0 all-gather.37
  1710.8 17.3 reduce-scatter.14
  1757.4 271.5 reduce-scatter.18
  2033.2 1177.4 reduce-scatter.16
